TPU v7x, 32 devices: a whole 2x2x4 slice. The times are simulated.
32 devices in a mesh: dp: 16 (over z, y, x), mp: 2 (over core).
Axes of the slice: x: 2, y: 2, z: 4, core: 2. Of those that a mesh axis runs over, the one named last changes fastest.
Arguments:
- grad: bfloat16 [4, 1024, 8192], P(None, 'dp', 'mp'), may hold values from -6 to 6
- second_moment: float32 [4, 1024, 8192], P(None, 'dp', 'mp'), may hold values from 0.004 to 20, as said below
- left_root: bfloat16 [2, 16, 1024, 1024], P('mp', 'dp'), as said below
- right_root: bfloat16 [2, 16, 1024, 1024], P('mp', 'dp'), as said below
- owner_slot: int32 [2, 4, 4], replicated, may hold values from 0 to 15, as said below
Outputs:
- update: bfloat16 [4, 1024, 8192], P(None, 'dp', 'mp')
Inputs may be any that keep to these rules, and one draw needn't show every extreme that they name: For each h, owner_slot[h] lists every dp index exactly once: each dp index owns one block of each h. `second_moment`: positive. `left_root`: each square is symmetric positive definite. `right_root`: each square is symmetric positive definite.
All inputs are finite; a program needn't handle non-finite values.
Results may differ from a plain program's by a relative error of at most 0.0049.
Values may be sent and summed in bfloat16 or wider, within the bound.
A program may use at most 64 MiB of HBM per device.

v0:
```python
import jax
import jax.numpy as jnp
from jax import lax
from jax.sharding import PartitionSpec as P

BETA_TWO = 0.99
ADAM_EPS = 1e-08
NORM_EPS = 1e-06


def per_device(grad, second_moment, left_root, right_root, owner_slot):
    row_blocks, block_rows, half_cols = grad.shape
    block_size = left_root.shape[-1]
    col_blocks = half_cols // block_size
    dp_count = lax.axis_size("dp")
    mp_index = lax.axis_index("mp")
    widened = grad.astype(jnp.float32)
    moment_new = BETA_TWO * second_moment + (1.0 - BETA_TWO) * widened * widened
    direction = widened / (jnp.sqrt(moment_new) + ADAM_EPS)
    partial_value = jnp.sum(
        (direction * direction).reshape(row_blocks, block_rows, col_blocks, block_size), axis=(1, 3)
    )
    table = lax.dynamic_index_in_dim(owner_slot, mp_index, 0, keepdims=False)
    owner_ids = lax.iota(jnp.int32, dp_count)
    matches = table[None, :, :] == owner_ids[:, None, None]
    select_half = matches.astype(jnp.bfloat16)
    select_full = matches.astype(jnp.float32).reshape(dp_count, row_blocks * col_blocks)
    tiles = grad.reshape(row_blocks, block_rows, col_blocks, block_size)
    outgoing = jnp.einsum("src,rwck->swk", select_half, tiles, preferred_element_type=jnp.float32)
    outgoing = outgoing.astype(jnp.bfloat16).reshape(dp_count, 1, block_rows, block_size)
    per_owner = jnp.dot(select_full, partial_value.reshape(-1), precision=lax.Precision.HIGHEST)
    arrived_sq = lax.all_to_all(per_owner, "dp", split_axis=0, concat_axis=0, tiled=True)
    adam_sq = jnp.sum(arrived_sq)
    left = left_root[0, 0]
    right = right_root[0, 0]
    arrived = lax.all_to_all(outgoing, "dp", split_axis=0, concat_axis=1, tiled=True)
    block = arrived.reshape(block_size, block_size)
    mixed = jnp.dot(block, right, preferred_element_type=jnp.float32).astype(jnp.bfloat16)
    shaped = jnp.dot(left, mixed, preferred_element_type=jnp.float32)
    shaped_sq = jnp.sum(shaped * shaped)
    factor = jnp.sqrt((adam_sq + NORM_EPS) / (shaped_sq + NORM_EPS))
    result = (shaped * factor).astype(jnp.bfloat16).reshape(1, dp_count, block_rows, block_size)
    back = lax.all_to_all(result, "dp", split_axis=1, concat_axis=0, tiled=True)
    placed = jnp.einsum(
        "src,swk->rwck",
        select_half,
        back.reshape(dp_count, block_rows, block_size),
        preferred_element_type=jnp.float32,
    )
    return placed.astype(jnp.bfloat16).reshape(row_blocks, block_rows, half_cols)


def solution(mesh):
    in_specs = (
        P(None, "dp", "mp"),
        P(None, "dp", "mp"),
        P("mp", "dp", None, None),
        P("mp", "dp", None, None),
        P(),
    )
    out_specs = P(None, "dp", "mp")
    return jax.shard_map(
        per_device, mesh=mesh, in_specs=in_specs, out_specs=out_specs, check_vma=False
    )
```

profile of v0, /device:TPU:0, one launch (start us, length us, event | category | flops | bytes accessed | tf_op | source)
XLA Modules:
  0.0 157.1 jit_solution(964478429440768154)
XLA Ops:
  0.0 0.0 copy-start
  0.0 0.0 copy-start.1
  0.0 5.4 %fusion.4 = f32[4,4096]{1,0:T(4,128)S(1)} fusion(f32[4,64,4096]{2,1,0:T(8,128)} %param.6, bf16[4,64,4096]{2,1,0:T(8,128)(2,1)} %param.5), kind=kLoop, calls=%fused_computation.9 | loop fusion | flops 9420800 | bytes 6356992 | tf_op jit(solution)/shard_map/reduce_sum | solution.py:20
  5.4 0.1 reduce_sum.35
  5.5 0.0 copy-done.1
  5.5 0.1 reduce_sum.36
  5.6 0.9 fusion.21
  6.5 8.3 %all-to-all-start.1 = ((f32[16,1,1]{2,1,0:T(1,128)}), f32[16,1,1]{2,1,0:T(1,128)S(1)}, u32[]{:S(2)}, u32[]{:S(2)}) async-start(f32[16,1,1]{2,1,0:T(1,128)} %bitcast.24), calls=%async_computation.1 | async-start | bytes 16384 | tf_op jit(solution)/shard_map/all_to_all | solution.py:32
  14.9 4.5 %reshape.32 = bf16[4,64,4,1024]{3,2,1,0:T(4,128)(2,1)} reshape(bf16[4,64,4096]{2,1,0:T(8,128)(2,1)} %param.5) | data formatting | bytes 4194304 | tf_op jit(solution)/shard_map/reshape | solution.py:28
  19.4 3.2 %fusion.15 = bf16[16,1,64,1024]{3,0,2,1:T(8,128)(2,1)S(1)} fusion(bf16[4,64,4,1024]{3,2,1,0:T(4,128)(2,1)} %reshape.32, s32[4,4]{1,0:T(4,128)S(1)} %dynamic-slice_bitcast_fusion), kind=kOutput, calls=%fused_computation.19 | convolution fusion | flops 34603264 | bytes 4194368 | tf_op jit(solution)/shard_map/src,rwck->swk/dot_general | solution.py:29
  22.6 2.5 %copy.22 = bf16[16,1,64,1024]{3,2,1,0:T(8,128)(2,1)} copy(bf16[16,1,64,1024]{3,0,2,1:T(8,128)(2,1)S(1)} %fusion.15) | data formatting | bytes 4194304 | tf_op jit(solution)/shard_map/reshape | solution.py:30
  25.1 0.0 all-to-all-done.1
  25.1 7.0 %all-to-all-start = ((bf16[16,1,64,1024]{3,2,1,0:T(8,128)(2,1)}), bf16[16,1,64,1024]{3,2,1,0:T(8,128)(2,1)}, u32[]{:S(2)}, u32[]{:S(2)}) async-start(bf16[16,1,64,1024]{3,2,1,0:T(8,128)(2,1)} %copy.22), calls=%async_computation | async-start | bytes 4194304 | tf_op jit(solution)/shard_map/all_to_all | solution.py:36
  32.0 0.7 reduce_sum.37
  33.4 41.4 %all-to-all-done = bf16[16,1,64,1024]{3,2,1,0:T(8,128)(2,1)} async-done(((bf16[16,1,64,1024]{3,2,1,0:T(8,128)(2,1)}), bf16[16,1,64,1024]{3,2,1,0:T(8,128)(2,1)}, u32[]{:S(2)}, u32[]{:S(2)}) %all-to-all-start) | async-done | bytes 2097184 | tf_op jit(solution)/shard_map/all_to_all | solution.py:36
  74.8 0.0 copy-done
  74.8 9.2 %multiply_reduce_fusion = (f32[]{:T(128)}, f32[1024,1024]{0,1:T(8,128)}) fusion(bf16[1024,1024]{1,0:T(8,128)(2,1)} %bitcast.5, bf16[1,1,1024,1024]{3,2,1,0:T(8,128)(2,1)S(1)} %copy-done, bf16[1,1,1024,1024]{3,2,1,0:T(8,128)(2,1)} %param.7), kind=kOutput, calls=%fused_computation.8 | convolution fusion | flops 4298113024 | bytes 10485764 | tf_op jit(solution)/shard_map/dot_general | solution.py:39
  84.8 2.8 %multiply_convert_fusion = bf16[1024,1024]{0,1:T(8,128)(2,1)S(1)} fusion(f32[1024,1024]{0,1:T(8,128)} %get-tuple-element.6, f32[]{:T(128)S(6)} %sqrt.7), kind=kLoop, calls=%fused_computation.7 | loop fusion | flops 2097152 | bytes 6291460 | tf_op jit(solution)/shard_map/convert_element_type | solution.py:42
  87.6 57.9 %all_to_all.27 = bf16[1,16,64,1024]{3,2,0,1:T(8,128)(2,1)S(1)} all-to-all(bf16[1,16,64,1024]{3,2,0,1:T(8,128)(2,1)S(1)} %bitcast.60), channel_id=1, replica_groups=mesh['dp'=16,'mp'=2] {'dp'}, dimensions={1} | all-to-all | bytes 4194304 | tf_op jit(solution)/shard_map/all_to_all | solution.py:43
  145.4 3.1 %convert_bitcast_fusion = bf16[4,64,4,1024]{3,2,0,1:T(4,128)(2,1)} fusion(bf16[1,16,64,1024]{3,2,0,1:T(8,128)(2,1)S(1)} %all_to_all.27, s32[4,4]{1,0:T(4,128)S(1)} %dynamic-slice_bitcast_fusion), kind=kOutput, calls=%fused_computation.17 | convolution fusion | flops 34603264 | bytes 4194368 | tf_op jit(solution)/shard_map/src,swk->rwck/dot_general | solution.py:44
  148.5 4.5 %reshape.37 = bf16[4,64,4096]{2,0,1:T(4,128)(2,1)} reshape(bf16[4,64,4,1024]{3,2,0,1:T(4,128)(2,1)} %convert_bitcast_fusion) | data formatting | bytes 4194304 | tf_op jit(solution)/shard_map/reshape | solution.py:50
  153.0 4.1 %copy.26 = bf16[4,64,4096]{2,1,0:T(8,128)(2,1)} copy(bf16[4,64,4096]{2,0,1:T(4,128)(2,1)} %reshape.37) | data formatting | bytes 4194304 | tf_op jit(solution)/shard_map/reshape | solution.py:50
  (1 shorter events, 0.0 us)
Async XLA Ops:
  0.0 74.8 %copy-start = (bf16[1,1,1024,1024]{3,2,1,0:T(8,128)(2,1)S(1)}, bf16[1,1,1024,1024]{3,2,1,0:T(8,128)(2,1)}, u32[]{:S(2)}) copy-start(bf16[1,1,1024,1024]{3,2,1,0:T(8,128)(2,1)} %param.8) | copy-start | bytes 6291460
  0.0 5.5 %copy-start.1 = (s32[2,4,4]{2,1,0:T(4,128)S(1)}, s32[2,4,4]{2,1,0:T(4,128)}, u32[]{:S(2)}) copy-start(s32[2,4,4]{2,1,0:T(4,128)} %param.9) | copy-start | bytes 388
  6.5 18.6 %all-to-all-start.1 = ((f32[16,1,1]{2,1,0:T(1,128)}), f32[16,1,1]{2,1,0:T(1,128)S(1)}, u32[]{:S(2)}, u32[]{:S(2)}) async-start(f32[16,1,1]{2,1,0:T(1,128)} %bitcast.24), calls=%async_computation.1 | async-start | bytes 16384 | tf_op jit(solution)/shard_map/all_to_all | solution.py:32
  25.1 49.7 %all-to-all-start = ((bf16[16,1,64,1024]{3,2,1,0:T(8,128)(2,1)}), bf16[16,1,64,1024]{3,2,1,0:T(8,128)(2,1)}, u32[]{:S(2)}, u32[]{:S(2)}) async-start(bf16[16,1,64,1024]{3,2,1,0:T(8,128)(2,1)} %copy.22), calls=%async_computation | async-start | bytes 4194304 | tf_op jit(solution)/shard_map/all_to_all | solution.py:36
where the time goes:
time: 158 us; the launch traced here: 157 us
  blocking collectives  57.9 us (37%)
  waiting for transfers between devices  41.4 us (26%)
  matrix products  16.5 us (10%)
  local copies, waits for them, and re-layouts  15.6 us (10%)
  starting transfers between devices  15.3 us (10%)
  other arithmetic  8.99 us (6%)
    all_to_all x1, blocking collectives, per_device(): back = lax.all_to_all(result, 'dp', split_axis=1, concat_axis=0, tiled=True)  57.9 us
    all_to_all x1, waiting for transfers between devices, per_device(): lax.all_to_all(outgoing, 'dp', split_axis=0, concat_axis=1, tiled=True)  41.4 us
    dot_general x1, matrix products, per_device(): shaped = jnp.dot(left, mixed, preferred_element_type=jnp.float32)  9.24 us
    reshape x2, local copies, waits for them, and re-layouts, per_device(): placed.astype(jnp.bfloat16).reshape(row_blocks, block_rows, half_cols)  8.57 us
    all_to_all x1, starting transfers between devices, per_device(): lax.all_to_all(per_owner, 'dp', split_axis=0, concat_axis=0, tiled=True)  8.34 us
    all_to_all x1, starting transfers between devices, per_device(): lax.all_to_all(outgoing, 'dp', split_axis=0, concat_axis=1, tiled=True)  6.96 us
    reduce_sum x2, other arithmetic, per_device(): jnp.sum((direction * direction).reshape(row_blocks, block_rows, col_block...  5.52 us
    reshape x1, local copies, waits for them, and re-layouts, per_device(): tiles = grad.reshape(row_blocks, block_rows, col_blocks, block_size)  4.49 us
  transfers between devices with their start and end apart: 2, of which 1 were waited for; matrix products, arithmetic and copies ran while one was open for 7% of the time, Pallas kernels for 0%

commit v1 on v0

--- a/solution.py
+++ b/solution.py
@@ -6,6 +6,28 @@
 BETA_TWO = 0.99
 ADAM_EPS = 1e-08
 NORM_EPS = 1e-06
+
+
+def in_blocks(x, dim, size):
+    before, after = (x.shape[:dim], x.shape[dim + 1 :])
+    return jnp.moveaxis(x.reshape(*before, size, -1, *after), dim, 0)
+
+
+def joined_along(blocks, dim):
+    lengths = list(blocks.shape[1:])
+    lengths[dim] *= blocks.shape[0]
+    return jnp.moveaxis(blocks, 0, dim).reshape(lengths)
+
+
+def exchange_in_pairs(shard, axis, split_dim, concat_dim):
+    size, here = (lax.axis_size(axis), lax.axis_index(axis))
+    blocks = in_blocks(shard, split_dim, size)
+    done = [blocks[here]]
+    for hop in range(1, size):
+        sent = blocks[here ^ hop]
+        done.append(lax.ppermute(sent, axis, [(i, i ^ hop) for i in range(size)]))
+    blocks = jnp.stack(done)[here ^ jnp.arange(size)]
+    return joined_along(blocks, concat_dim)
 
 
 def per_device(grad, second_moment, left_root, right_root, owner_slot):
@@ -33,7 +55,7 @@
     adam_sq = jnp.sum(arrived_sq)
     left = left_root[0, 0]
     right = right_root[0, 0]
-    arrived = lax.all_to_all(outgoing, "dp", split_axis=0, concat_axis=1, tiled=True)
+    arrived = exchange_in_pairs(outgoing, "dp", 0, 1)
     block = arrived.reshape(block_size, block_size)
     mixed = jnp.dot(block, right, preferred_element_type=jnp.float32).astype(jnp.bfloat16)
     shaped = jnp.dot(left, mixed, preferred_element_type=jnp.float32)

time: 158 us -> 181 us (1.15)
  waiting for transfers between devices: 41.4 us -> 7.92 us
  local copies, waits for them, and re-layouts: 15.6 us -> 45.5 us
  starting transfers between devices: 15.3 us -> 41.1 us
    all_to_all x1 -> x0, waiting for transfers between devices: 41.4 us -> none  [per_device(): lax.all_to_all(outgoing, 'dp', split_axis=0, concat_axis=1, tiled=True)]
    ppermute x0 -> x15, starting transfers between devices: none -> 32.7 us  [exchange_in_pairs(): done.append(lax.ppermute(sent, axis, [(i, i ^ hop) for i in range(size)]))]
    unnamed x4 -> x34, local copies, waits for them, and re-layouts: 0.01 us -> 17.8 us
    dynamic_slice x0 -> x1, local copies, waits for them, and re-layouts: none -> 10.4 us  [exchange_in_pairs(): sent = blocks[here ^ hop]]
    ppermute x0 -> x15, waiting for transfers between devices: none -> 7.91 us  [exchange_in_pairs(): done.append(lax.ppermute(sent, axis, [(i, i ^ hop) for i in range(size)]))]
    all_to_all x1 -> x0, starting transfers between devices: 6.96 us -> none  [per_device(): lax.all_to_all(outgoing, 'dp', split_axis=0, concat_axis=1, tiled=True)]
    gather x0 -> x1, local copies, waits for them, and re-layouts: none -> 3.59 us  [exchange_in_pairs(): blocks = jnp.stack(done)[here ^ jnp.arange(size)]]
    reshape x1 -> x0, local copies, waits for them, and re-layouts: 2.47 us -> none  [per_device(): outgoing.astype(jnp.bfloat16).reshape(dp_count, 1, block_rows, block_size)]
  transfers between devices with their start and end apart: 2 -> 16, of which waited for: 1 -> 2; matrix products, arithmetic and copies ran while one was open for 7% -> 21% of each run, Pallas kernels for 0% -> 0%
where the time goes in v1:
time: 181 us
  blocking collectives  57.9 us (32%)
  local copies, waits for them, and re-layouts  45.5 us (25%)
  starting transfers between devices  41.1 us (23%)
  matrix products  17.8 us (10%)
  other arithmetic  8.99 us (5%)
  waiting for transfers between devices  7.92 us (4%)
    all_to_all x1, blocking collectives, per_device(): back = lax.all_to_all(result, 'dp', split_axis=1, concat_axis=0, tiled=True)  57.9 us
    ppermute x15, starting transfers between devices, exchange_in_pairs(): done.append(lax.ppermute(sent, axis, [(i, i ^ hop) for i in range(size)]))  32.7 us
    unnamed x34, local copies, waits for them, and re-layouts  17.8 us
    dynamic_slice x1, local copies, waits for them, and re-layouts, exchange_in_pairs(): sent = blocks[here ^ hop]  10.4 us
    dot_general x1, matrix products, per_device(): shaped = jnp.dot(left, mixed, preferred_element_type=jnp.float32)  9.26 us
    reshape x2, local copies, waits for them, and re-layouts, per_device(): placed.astype(jnp.bfloat16).reshape(row_blocks, block_rows, half_cols)  8.56 us
    all_to_all x1, starting transfers between devices, per_device(): lax.all_to_all(per_owner, 'dp', split_axis=0, concat_axis=0, tiled=True)  8.35 us
    ppermute x15, waiting for transfers between devices, exchange_in_pairs(): done.append(lax.ppermute(sent, axis, [(i, i ^ hop) for i in range(size)]))  7.91 us
  transfers between devices with their start and end apart: 16, of which 2 were waited for; matrix products, arithmetic and copies ran while one was open for 21% of the time, Pallas kernels for 0%

profile of v1, /device:TPU:0, one launch (start us, length us, event | category | flops | bytes accessed | tf_op | source)
XLA Modules:
  0.0 180.9 jit_solution(8874958792570150682)
XLA Ops:
  0.0 5.4 %fusion.4 = f32[4,4096]{1,0:T(4,128)S(1)} fusion(f32[4,64,4096]{2,1,0:T(8,128)} %param.6, bf16[4,64,4096]{2,1,0:T(8,128)(2,1)} %param.5), kind=kLoop, calls=%fused_computation.10 | loop fusion | flops 9420800 | bytes 6356992 | tf_op jit(solution)/shard_map/reduce_sum | solution.py:42
  5.6 0.9 fusion.20
  6.5 8.3 %all-to-all-start = ((f32[16,1,1]{2,1,0:T(1,128)}), f32[16,1,1]{2,1,0:T(1,128)S(1)}, u32[]{:S(2)}, u32[]{:S(2)}) async-start(f32[16,1,1]{2,1,0:T(1,128)} %bitcast.56), calls=%async_computation | async-start | bytes 16384 | tf_op jit(solution)/shard_map/all_to_all | solution.py:54
  14.9 4.5 %reshape.69 = bf16[4,64,4,1024]{3,2,1,0:T(4,128)(2,1)} reshape(bf16[4,64,4096]{2,1,0:T(8,128)(2,1)} %param.5) | data formatting | bytes 4194304 | tf_op jit(solution)/shard_map/reshape | solution.py:50
  19.4 4.6 %bitcast_convert_fusion = bf16[16,64,1024]{2,0,1:T(8,128)(2,1)} fusion(bf16[4,64,4,1024]{3,2,1,0:T(4,128)(2,1)} %reshape.69, s32[4,4]{1,0:T(4,128)S(1)} %fusion.27), kind=kOutput, calls=%fused_computation.7 | convolution fusion | flops 34603264 | bytes 4194368 | tf_op jit(solution)/shard_map/src,rwck->swk/dot_general | solution.py:51
  24.0 10.4 %constant_dynamic-slice_fusion = (bf16[1,64,1024]{2,0,1:T(2,128)(2,1)S(1)}, bf16[1,64,1024]{2,0,1:T(2,128)(2,1)S(1)}, bf16[1,64,1024]{2,0,1:T(2,128)(2,1)S(1)}, ...) fusion(bf16[16,64,1024]{2,0,1:T(8,128)(2,1)} %bitcast_convert_f, ...), kind=kLoop, calls=%fused_computation.55 | loop fusion | bytes 4194368 | tf_op jit(solution)/shard_map/dynamic_slice | solution.py:27
  34.4 0.7 copy.79
  35.1 1.8 %collective-permute-start = (bf16[1,1,64,1024]{3,2,1,0:T(8,128)(2,1)}, bf16[1,1,64,1024]{3,2,1,0:T(8,128)(2,1)}, u32[]{:S(2)}, u32[]{:S(2)}) collective-permute-start(bf16[1,1,64,1024]{3,2,1,0:T(8,128)(2,1)} %bitcast.135), channel_id=1, source_target_pairs={{0,2},{2,0},{4,6},{6,4},{8,10},{10,8},{12,14},{14,12},{16,18},{18,... | collective-permute-start | bytes 393224 | tf_op jit(solution)/shard_map/ppermute | solution.py:28
  36.9 0.7 copy.78
  37.6 1.5 collective-permute-start.1
  39.1 0.7 copy.77
  40.0 1.9 %collective-permute-start.3 = (bf16[1,1,64,1024]{3,2,1,0:T(8,128)(2,1)S(1)}, bf16[1,1,64,1024]{3,2,1,0:T(8,128)(2,1)}, u32[]{:S(2)}, u32[]{:S(2)}) collective-permute-start(bf16[1,1,64,1024]{3,2,1,0:T(8,128)(2,1)S(1)} %bitcast.149), channel_id=1, source_target_pairs={{0,8},{2,10},{4,12},{6,14},{8,0},{10,2},{12,4},{14,6},{16,24},{18,... | collective-permute-start | bytes 393224 | tf_op jit(solution)/shard_map/ppermute | solution.py:28
  42.0 1.5 collective-permute-start.4
  43.5 0.7 bitcast_dynamic-update-slice_fusion
  44.7 0.7 copy.74
  45.4 0.7 reduce_sum.37
  46.8 2.4 %collective-permute-start.5 = (bf16[1,1,64,1024]{3,2,1,0:T(8,128)(2,1)}, bf16[1,1,64,1024]{3,2,1,0:T(8,128)(2,1)S(1)}, u32[]{:S(2)}, u32[]{:S(2)}) collective-permute-start(bf16[1,1,64,1024]{3,2,1,0:T(8,128)(2,1)} %bitcast.150), channel_id=1, source_target_pairs={{0,12},{2,14},{4,8},{6,10},{8,4},{10,6},{12,0},{14,2},{16,28},{18,... | collective-permute-start | bytes 393224 | tf_op jit(solution)/shard_map/ppermute | solution.py:28
  49.2 1.6 bitcast_dynamic-update-slice_fusion.15
  50.9 1.6 bitcast_dynamic-update-slice_fusion.14
  52.5 2.8 %collective-permute-start.7 = (bf16[1,1,64,1024]{3,2,1,0:T(8,128)(2,1)S(1)}, bf16[1,1,64,1024]{3,2,1,0:T(8,128)(2,1)S(1)}, u32[]{:S(2)}, u32[]{:S(2)}) collective-permute-start(bf16[1,1,64,1024]{3,2,1,0:T(8,128)(2,1)S(1)} %bitcast.146), channel_id=1, source_target_pairs={{0,16},{2,18},{4,20},{6,22},{8,24},{10,26},{12,28},{14,30},{16,0},... | collective-permute-start | bytes 393224 | tf_op jit(solution)/shard_map/ppermute | solution.py:28
  55.3 1.6 bitcast_dynamic-update-slice_fusion.13
  56.8 1.5 collective-permute-start.8
  58.3 1.6 bitcast_dynamic-update-slice_fusion.12
  59.9 3.3 %collective-permute-start.9 = (bf16[1,1,64,1024]{3,2,1,0:T(8,128)(2,1)S(1)}, bf16[1,1,64,1024]{3,2,1,0:T(8,128)(2,1)S(1)}, u32[]{:S(2)}, u32[]{:S(2)}) collective-permute-start(bf16[1,1,64,1024]{3,2,1,0:T(8,128)(2,1)S(1)} %bitcast.144), channel_id=1, source_target_pairs={{0,20},{2,22},{4,16},{6,18},{8,28},{10,30},{12,24},{14,26},{16,4},... | collective-permute-start | bytes 393224 | tf_op jit(solution)/shard_map/ppermute | solution.py:28
  63.1 1.6 bitcast_dynamic-update-slice_fusion.11
  64.9 0.7 bitcast_dynamic-update-slice_fusion.10
  65.5 3.7 %collective-permute-start.11 = (bf16[1,1,64,1024]{3,2,1,0:T(8,128)(2,1)S(1)}, bf16[1,1,64,1024]{3,2,1,0:T(8,128)(2,1)S(1)}, u32[]{:S(2)}, u32[]{:S(2)}) collective-permute-start(bf16[1,1,64,1024]{3,2,1,0:T(8,128)(2,1)S(1)} %bitcast.142), channel_id=1, source_target_pairs={{0,24},{2,26},{4,28},{6,30},{8,16},{10,18},{12,20},{14,22},{16,8},... | collective-permute-start | bytes 393224 | tf_op jit(solution)/shard_map/ppermute | solution.py:28
  69.2 0.7 bitcast_dynamic-update-slice_fusion.9
  69.9 7.5 %collective-permute-start.12 = (bf16[1,1,64,1024]{3,2,1,0:T(8,128)(2,1)S(1)}, bf16[1,1,64,1024]{3,2,1,0:T(8,128)(2,1)S(1)}, u32[]{:S(2)}, u32[]{:S(2)}) collective-permute-start(bf16[1,1,64,1024]{3,2,1,0:T(8,128)(2,1)S(1)} %bitcast.141), channel_id=1, source_target_pairs={{0,26},{2,24},{4,30},{6,28},{8,18},{10,16},{12,22},{14,20},{16,10}... | collective-permute-start | bytes 393224 | tf_op jit(solution)/shard_map/ppermute | solution.py:28
  77.3 0.7 bitcast_dynamic-update-slice_fusion.8
  78.0 3.0 %collective-permute-start.13 = (bf16[1,1,64,1024]{3,2,1,0:T(8,128)(2,1)S(1)}, bf16[1,1,64,1024]{3,2,1,0:T(8,128)(2,1)S(1)}, u32[]{:S(2)}, u32[]{:S(2)}) collective-permute-start(bf16[1,1,64,1024]{3,2,1,0:T(8,128)(2,1)S(1)} %bitcast.140), channel_id=1, source_target_pairs={{0,28},{2,30},{4,24},{6,26},{8,20},{10,22},{12,16},{14,18},{16,12}... | collective-permute-start | bytes 393224 | tf_op jit(solution)/shard_map/ppermute | solution.py:28
  81.0 0.7 bitcast_dynamic-update-slice_fusion.7
  81.7 0.9 collective-permute-done.9
  82.6 1.3 collective-permute-start.14
  84.0 0.7 bitcast_dynamic-update-slice_fusion.6
  84.6 7.0 %collective-permute-done.10 = bf16[1,1,64,1024]{3,2,1,0:T(8,128)(2,1)S(1)} collective-permute-done((bf16[1,1,64,1024]{3,2,1,0:T(8,128)(2,1)S(1)}, bf16[1,1,64,1024]{3,2,1,0:T(8,128)(2,1)S(1)}, u32[]{:S(2)}, u32[]{:S(2)}) %collective-permute-start.10) | collective-permute-done | bytes 131104 | tf_op jit(solution)/shard_map/ppermute | solution.py:28
  91.6 0.7 bitcast_dynamic-update-slice_fusion.5
  92.3 0.7 bitcast_dynamic-update-slice_fusion.4
  92.9 0.7 bitcast_dynamic-update-slice_fusion.3
  93.6 0.7 bitcast_dynamic-update-slice_fusion.2
  94.3 0.7 bitcast_dynamic-update-slice_fusion.1
  94.9 3.6 %gather_fusion = bf16[16,64,1024]{2,1,0:T(8,128)(2,1)} fusion(bf16[16,64,1024]{2,1,0:T(8,128)(2,1)} %bitcast.137, s32[1024]{0:T(1024)S(1)} %pad_clamp_fusion), kind=kCustom, calls=%fused_computation | custom fusion | bytes 4194368 | tf_op jit(solution)/shard_map/gather | solution.py:29
  98.5 9.3 %multiply_reduce_fusion = (f32[]{:T(128)}, f32[1024,1024]{0,1:T(8,128)}) fusion(bf16[1024,1024]{1,0:T(8,128)(2,1)} %bitcast.138, bf16[1,1,1024,1024]{3,2,1,0:T(8,128)(2,1)S(1)} %copy-done, bf16[1,1,1024,1024]{3,2,1,0:T(8,128)(2,1)} %param.7), kind=kOutput, calls=%fused_computation.9 | convolution fusion | flops 4298113024 | bytes 10485764 | tf_op jit(solution)/shard_map/dot_general | solution.py:61
  108.5 2.8 %multiply_convert_fusion = bf16[1024,1024]{0,1:T(8,128)(2,1)S(1)} fusion(f32[1024,1024]{0,1:T(8,128)} %get-tuple-element.22, f32[]{:T(128)S(6)} %sqrt.7), kind=kLoop, calls=%fused_computation.8 | loop fusion | flops 2097152 | bytes 6291460 | tf_op jit(solution)/shard_map/convert_element_type | solution.py:64
  111.3 57.9 %all_to_all.18 = bf16[1,16,64,1024]{3,2,0,1:T(8,128)(2,1)S(1)} all-to-all(bf16[1,16,64,1024]{3,2,0,1:T(8,128)(2,1)S(1)} %bitcast.136), channel_id=1, replica_groups=mesh['dp'=16,'mp'=2] {'dp'}, dimensions={1} | all-to-all | bytes 4194304 | tf_op jit(solution)/shard_map/all_to_all | solution.py:65
  169.2 3.1 %convert_bitcast_fusion = bf16[4,64,4,1024]{3,2,0,1:T(4,128)(2,1)} fusion(bf16[1,16,64,1024]{3,2,0,1:T(8,128)(2,1)S(1)} %all_to_all.18, s32[4,4]{1,0:T(4,128)S(1)} %fusion.27), kind=kOutput, calls=%fused_computation.18 | convolution fusion | flops 34603264 | bytes 4194368 | tf_op jit(solution)/shard_map/src,swk->rwck/dot_general | solution.py:66
  172.3 4.5 %reshape.72 = bf16[4,64,4096]{2,0,1:T(4,128)(2,1)} reshape(bf16[4,64,4,1024]{3,2,0,1:T(4,128)(2,1)} %convert_bitcast_fusion) | data formatting | bytes 4194304 | tf_op jit(solution)/shard_map/reshape | solution.py:72
  176.8 4.1 %copy.23 = bf16[4,64,4096]{2,1,0:T(8,128)(2,1)} copy(bf16[4,64,4096]{2,0,1:T(4,128)(2,1)} %reshape.72) | data formatting | bytes 4194304 | tf_op jit(solution)/shard_map/reshape | solution.py:72
  (37 shorter events, 1.2 us)
Async XLA Ops:
  0.0 98.5 %copy-start = (bf16[1,1,1024,1024]{3,2,1,0:T(8,128)(2,1)S(1)}, bf16[1,1,1024,1024]{3,2,1,0:T(8,128)(2,1)}, u32[]{:S(2)}) copy-start(bf16[1,1,1024,1024]{3,2,1,0:T(8,128)(2,1)} %param.8) | copy-start | bytes 6291460
  0.0 5.5 %copy-start.1 = (s32[2,4,4]{2,1,0:T(4,128)S(1)}, s32[2,4,4]{2,1,0:T(4,128)}, u32[]{:S(2)}) copy-start(s32[2,4,4]{2,1,0:T(4,128)} %param.9) | copy-start | bytes 388
  6.5 38.9 %all-to-all-start = ((f32[16,1,1]{2,1,0:T(1,128)}), f32[16,1,1]{2,1,0:T(1,128)S(1)}, u32[]{:S(2)}, u32[]{:S(2)}) async-start(f32[16,1,1]{2,1,0:T(1,128)} %bitcast.56), calls=%async_computation | async-start | bytes 16384 | tf_op jit(solution)/shard_map/all_to_all | solution.py:54
  35.1 11.7 %collective-permute-start = (bf16[1,1,64,1024]{3,2,1,0:T(8,128)(2,1)}, bf16[1,1,64,1024]{3,2,1,0:T(8,128)(2,1)}, u32[]{:S(2)}, u32[]{:S(2)}) collective-permute-start(bf16[1,1,64,1024]{3,2,1,0:T(8,128)(2,1)} %bitcast.135), channel_id=1, source_target_pairs={{0,2},{2,0},{4,6},{6,4},{8,10},{10,8},{12,14},{14,12},{16,18},{18,... | collective-permute-start | bytes 393224 | tf_op jit(solution)/shard_map/ppermute | solution.py:28
  37.6 13.1 %collective-permute-start.1 = (bf16[1,1,64,1024]{3,2,1,0:T(8,128)(2,1)}, bf16[1,1,64,1024]{3,2,1,0:T(8,128)(2,1)}, u32[]{:S(2)}, u32[]{:S(2)}) collective-permute-start(bf16[1,1,64,1024]{3,2,1,0:T(8,128)(2,1)} %bitcast.134), channel_id=1, source_target_pairs={{0,4},{2,6},{4,0},{6,2},{8,12},{10,14},{12,8},{14,10},{16,20},{18,... | collective-permute-start | bytes 393224 | tf_op jit(solution)/shard_map/ppermute | solution.py:28
  39.8 12.7 %collective-permute-start.2 = (bf16[1,1,64,1024]{3,2,1,0:T(8,128)(2,1)}, bf16[1,1,64,1024]{3,2,1,0:T(8,128)(2,1)}, u32[]{:S(2)}, u32[]{:S(2)}) collective-permute-start(bf16[1,1,64,1024]{3,2,1,0:T(8,128)(2,1)} %bitcast.133), channel_id=1, source_target_pairs={{0,6},{2,4},{4,2},{6,0},{8,14},{10,12},{12,10},{14,8},{16,22},{18,... | collective-permute-start | bytes 393224 | tf_op jit(solution)/shard_map/ppermute | solution.py:28
  40.0 16.8 %collective-permute-start.3 = (bf16[1,1,64,1024]{3,2,1,0:T(8,128)(2,1)S(1)}, bf16[1,1,64,1024]{3,2,1,0:T(8,128)(2,1)}, u32[]{:S(2)}, u32[]{:S(2)}) collective-permute-start(bf16[1,1,64,1024]{3,2,1,0:T(8,128)(2,1)S(1)} %bitcast.149), channel_id=1, source_target_pairs={{0,8},{2,10},{4,12},{6,14},{8,0},{10,2},{12,4},{14,6},{16,24},{18,... | collective-permute-start | bytes 393224 | tf_op jit(solution)/shard_map/ppermute | solution.py:28
  42.0 17.9 %collective-permute-start.4 = (bf16[1,1,64,1024]{3,2,1,0:T(8,128)(2,1)S(1)}, bf16[1,1,64,1024]{3,2,1,0:T(8,128)(2,1)}, u32[]{:S(2)}, u32[]{:S(2)}) collective-permute-start(bf16[1,1,64,1024]{3,2,1,0:T(8,128)(2,1)S(1)} %bitcast.147), channel_id=1, source_target_pairs={{0,10},{2,8},{4,14},{6,12},{8,2},{10,0},{12,6},{14,4},{16,26},{18,... | collective-permute-start | bytes 393224 | tf_op jit(solution)/shard_map/ppermute | solution.py:28
  46.8 17.9 %collective-permute-start.5 = (bf16[1,1,64,1024]{3,2,1,0:T(8,128)(2,1)}, bf16[1,1,64,1024]{3,2,1,0:T(8,128)(2,1)S(1)}, u32[]{:S(2)}, u32[]{:S(2)}) collective-permute-start(bf16[1,1,64,1024]{3,2,1,0:T(8,128)(2,1)} %bitcast.150), channel_id=1, source_target_pairs={{0,12},{2,14},{4,8},{6,10},{8,4},{10,6},{12,0},{14,2},{16,28},{18,... | collective-permute-start | bytes 393224 | tf_op jit(solution)/shard_map/ppermute | solution.py:28
  50.8 14.8 %collective-permute-start.6 = (bf16[1,1,64,1024]{3,2,1,0:T(8,128)(2,1)S(1)}, bf16[1,1,64,1024]{3,2,1,0:T(8,128)(2,1)S(1)}, u32[]{:S(2)}, u32[]{:S(2)}) collective-permute-start(bf16[1,1,64,1024]{3,2,1,0:T(8,128)(2,1)S(1)} %bitcast.148), channel_id=1, source_target_pairs={{0,14},{2,12},{4,10},{6,8},{8,6},{10,4},{12,2},{14,0},{16,30},{18,... | collective-permute-start | bytes 393224 | tf_op jit(solution)/shard_map/ppermute | solution.py:28
  52.5 17.4 %collective-permute-start.7 = (bf16[1,1,64,1024]{3,2,1,0:T(8,128)(2,1)S(1)}, bf16[1,1,64,1024]{3,2,1,0:T(8,128)(2,1)S(1)}, u32[]{:S(2)}, u32[]{:S(2)}) collective-permute-start(bf16[1,1,64,1024]{3,2,1,0:T(8,128)(2,1)S(1)} %bitcast.146), channel_id=1, source_target_pairs={{0,16},{2,18},{4,20},{6,22},{8,24},{10,26},{12,28},{14,30},{16,0},... | collective-permute-start | bytes 393224 | tf_op jit(solution)/shard_map/ppermute | solution.py:28
  56.8 21.2 %collective-permute-start.8 = (bf16[1,1,64,1024]{3,2,1,0:T(8,128)(2,1)S(1)}, bf16[1,1,64,1024]{3,2,1,0:T(8,128)(2,1)S(1)}, u32[]{:S(2)}, u32[]{:S(2)}) collective-permute-start(bf16[1,1,64,1024]{3,2,1,0:T(8,128)(2,1)S(1)} %bitcast.145), channel_id=1, source_target_pairs={{0,18},{2,16},{4,22},{6,20},{8,26},{10,24},{12,30},{14,28},{16,2},... | collective-permute-start | bytes 393224 | tf_op jit(solution)/shard_map/ppermute | solution.py:28
  59.9 22.8 %collective-permute-start.9 = (bf16[1,1,64,1024]{3,2,1,0:T(8,128)(2,1)S(1)}, bf16[1,1,64,1024]{3,2,1,0:T(8,128)(2,1)S(1)}, u32[]{:S(2)}, u32[]{:S(2)}) collective-permute-start(bf16[1,1,64,1024]{3,2,1,0:T(8,128)(2,1)S(1)} %bitcast.144), channel_id=1, source_target_pairs={{0,20},{2,22},{4,16},{6,18},{8,28},{10,30},{12,24},{14,26},{16,4},... | collective-permute-start | bytes 393224 | tf_op jit(solution)/shard_map/ppermute | solution.py:28
  64.7 26.9 %collective-permute-start.10 = (bf16[1,1,64,1024]{3,2,1,0:T(8,128)(2,1)S(1)}, bf16[1,1,64,1024]{3,2,1,0:T(8,128)(2,1)S(1)}, u32[]{:S(2)}, u32[]{:S(2)}) collective-permute-start(bf16[1,1,64,1024]{3,2,1,0:T(8,128)(2,1)S(1)} %bitcast.143), channel_id=1, source_target_pairs={{0,22},{2,20},{4,18},{6,16},{8,30},{10,28},{12,26},{14,24},{16,6},... | collective-permute-start | bytes 393224 | tf_op jit(solution)/shard_map/ppermute | solution.py:28
  65.5 26.7 %collective-permute-start.11 = (bf16[1,1,64,1024]{3,2,1,0:T(8,128)(2,1)S(1)}, bf16[1,1,64,1024]{3,2,1,0:T(8,128)(2,1)S(1)}, u32[]{:S(2)}, u32[]{:S(2)}) collective-permute-start(bf16[1,1,64,1024]{3,2,1,0:T(8,128)(2,1)S(1)} %bitcast.142), channel_id=1, source_target_pairs={{0,24},{2,26},{4,28},{6,30},{8,16},{10,18},{12,20},{14,22},{16,8},... | collective-permute-start | bytes 393224 | tf_op jit(solution)/shard_map/ppermute | solution.py:28
  69.9 23.1 %collective-permute-start.12 = (bf16[1,1,64,1024]{3,2,1,0:T(8,128)(2,1)S(1)}, bf16[1,1,64,1024]{3,2,1,0:T(8,128)(2,1)S(1)}, u32[]{:S(2)}, u32[]{:S(2)}) collective-permute-start(bf16[1,1,64,1024]{3,2,1,0:T(8,128)(2,1)S(1)} %bitcast.141), channel_id=1, source_target_pairs={{0,26},{2,24},{4,30},{6,28},{8,18},{10,16},{12,22},{14,20},{16,10}... | collective-permute-start | bytes 393224 | tf_op jit(solution)/shard_map/ppermute | solution.py:28
  78.0 15.6 %collective-permute-start.13 = (bf16[1,1,64,1024]{3,2,1,0:T(8,128)(2,1)S(1)}, bf16[1,1,64,1024]{3,2,1,0:T(8,128)(2,1)S(1)}, u32[]{:S(2)}, u32[]{:S(2)}) collective-permute-start(bf16[1,1,64,1024]{3,2,1,0:T(8,128)(2,1)S(1)} %bitcast.140), channel_id=1, source_target_pairs={{0,28},{2,30},{4,24},{6,26},{8,20},{10,22},{12,16},{14,18},{16,12}... | collective-permute-start | bytes 393224 | tf_op jit(solution)/shard_map/ppermute | solution.py:28
  82.6 11.6 %collective-permute-start.14 = (bf16[1,1,64,1024]{3,2,1,0:T(8,128)(2,1)S(1)}, bf16[1,1,64,1024]{3,2,1,0:T(8,128)(2,1)S(1)}, u32[]{:S(2)}, u32[]{:S(2)}) collective-permute-start(bf16[1,1,64,1024]{3,2,1,0:T(8,128)(2,1)S(1)} %bitcast.139), channel_id=1, source_target_pairs={{0,30},{2,28},{4,26},{6,24},{8,22},{10,20},{12,18},{14,16},{16,14}... | collective-permute-start | bytes 393224 | tf_op jit(solution)/shard_map/ppermute | solution.py:28
